TPU v7x, 32 devices: a whole 2x2x4 slice. The times are simulated.
32 devices in a mesh: row: 4 (over y, x), col: 8 (over z, core).
Axes of the slice: x: 2, y: 2, z: 4, core: 2. Of those that a mesh axis runs over, the one named last changes fastest.
Arguments:
- tokens: bfloat16 [4096, 2048], P(('row', 'col')), may hold values from -6 to 6
- expert_ids: int32 [4096, 8], P(('row', 'col')), may hold values from 0 to 31, all different within a row; in each aligned block of 128 rows (0 to 127, 128 to 255, ...) at most 40 rows name the same one
- gate_probs: float32 [4096, 8], P(('row', 'col')), may hold values from 0.05 to 0.5
- w_gate: bfloat16 [32, 2048, 768], P(('row', 'col')), may hold values from -0.125 to 0.125
- w_up: bfloat16 [32, 2048, 768], P(('row', 'col')), may hold values from -0.125 to 0.125
- w_down: bfloat16 [32, 768, 2048], P(('row', 'col')), may hold values from -0.21875 to 0.21875
Outputs:
- mixed: bfloat16 [4096, 2048], P(('row', 'col'))
Inputs may be any that keep to these rules, and one draw needn't show every extreme that they name: `expert_ids`: each row names 8 different experts; among the rows of one device (aligned blocks of 128 rows) no expert is named more than 40 times.
All inputs are finite; a program needn't handle non-finite values.
Results may differ from a plain program's by a relative error of at most 0.0058.
Values may be sent and summed in bfloat16 or wider, within the bound.
A program may use at most 128 MiB of HBM per device.

v0:
```python
import jax
import jax.numpy as jnp
from jax import lax
from jax.sharding import PartitionSpec as P


def apply_experts(received, w_gate, w_up, w_down):
    width = received.shape[-1]
    rows = received[:, 0].reshape(-1, width)
    gate = jnp.dot(rows, w_gate[0], preferred_element_type=jnp.float32)
    up = jnp.dot(rows, w_up[0], preferred_element_type=jnp.float32)
    hidden = (jax.nn.silu(gate) * up).astype(jnp.bfloat16)
    result = jnp.dot(hidden, w_down[0], preferred_element_type=jnp.float32).astype(jnp.bfloat16)
    results = [result.reshape(received.shape[0], received.shape[2], width)]
    return jnp.stack(results, axis=1)


def body(tokens, expert_ids, gate_probs, w_gate, w_up, w_down):
    tok_rows, choices_per = expert_ids.shape
    width = tokens.shape[1]
    rows_axis = lax.axis_size("row")
    cols_axis = lax.axis_size("col")
    devices_all = rows_axis * cols_axis
    local_count = w_gate.shape[0]
    expert_count = local_count * devices_all
    slot_count = 5 * tok_rows * choices_per // (4 * expert_count)
    flat_ids = expert_ids.reshape(-1)
    onehot = (flat_ids[:, None] == jnp.arange(expert_count, dtype=jnp.int32)[None, :]).astype(
        jnp.int32
    )
    rank = jnp.sum((jnp.cumsum(onehot, axis=0) - 1) * onehot, axis=1)
    target = flat_ids * slot_count + rank
    repeated = jnp.repeat(tokens, choices_per, axis=0)
    buffer = jnp.zeros((expert_count * slot_count, width), jnp.bfloat16).at[target].set(repeated)
    outgoing = buffer.reshape(devices_all, local_count, slot_count, width)
    produced = apply_experts(
        lax.all_to_all(outgoing, ("row", "col"), split_axis=0, concat_axis=0, tiled=True),
        w_gate,
        w_up,
        w_down,
    )
    returned = lax.all_to_all(produced, ("row", "col"), split_axis=0, concat_axis=0, tiled=True)
    returned = returned.reshape(expert_count * slot_count, width)
    picked = returned[target].reshape(tok_rows, choices_per, width).astype(jnp.float32)
    mixed = jnp.sum(gate_probs[:, :, None] * picked, axis=1)
    return mixed.astype(jnp.bfloat16)


def solution(mesh):
    in_specs = (
        P(("row", "col"), None),
        P(("row", "col"), None),
        P(("row", "col"), None),
        P(("row", "col"), None, None),
        P(("row", "col"), None, None),
        P(("row", "col"), None, None),
    )
    out_specs = P(("row", "col"), None)
    return jax.shard_map(body, mesh=mesh, in_specs=in_specs, out_specs=out_specs, check_vma=False)
```

profile of v0, /device:TPU:0, one launch (start us, length us, event | category | flops | bytes accessed | tf_op | source)
XLA Modules:
  0.0 302.0 jit_solution(2987483357552669853)
XLA Ops:
  0.0 0.0 copy-start
  0.0 0.9 copy.16
  0.9 0.1 eq.29
  1.0 0.1 eq.25
  1.1 0.7 broadcast_multiply_fusion
  1.8 9.0 %reduce-window.6 = s32[32,8,128]{2,1,0:T(8,128)S(1)} reduce-window(s32[32,8,128]{2,1,0:T(8,128)S(1)} %fusion.12, s32[]{:T(128)} %constant.9.clone.1), window={size=1x1x128 pad=0_0x0_0x127_0}, to_apply=%region_0.0 | reduce-window | flops 4161536 | bytes 262148 | tf_op jit(solution)/shard_map/reduce-window
  10.8 0.1 slice.10
  10.9 0.1 copy.18
  11.1 0.1 copy.19
  11.2 0.1 add_add_fusion
  11.3 0.1 copy.15
  11.4 0.1 mul.37
  11.6 10.1 %scatter_custom_fusion = bf16[1280,2048]{1,0:T(8,128)(2,1)} fusion(s32[1024]{0:T(1024)S(1)} %bitcast.47, bf16[]{:T(256)} %constant.7.clone.1, bf16[128,2048]{1,0:T(8,128)(2,1)} %param.6), kind=kCustom, calls=%fused_computation.5 | custom fusion | bytes 5767170 | tf_op jit(solution)/shard_map/scatter | solution.py:34
  21.6 124.7 %all_to_all.10 = bf16[32,1,40,2048]{3,2,1,0:T(8,128)(2,1)S(1)} all-to-all(bf16[32,1,40,2048]{3,2,1,0:T(8,128)(2,1)} %bitcast.40), channel_id=1, replica_groups=mesh['row'=4,'col'=8] {'row','col'}, dimensions={0} | all-to-all | bytes 10485760 | tf_op jit(solution)/shard_map/all_to_all | solution.py:37
  146.3 0.0 copy-done.2
  146.3 4.3 %fusion.6 = f32[1280,768]{1,0:T(8,128)S(1)} fusion(bf16[1280,2048]{1,0:T(8,128)(2,1)S(1)} %bitcast.42, bf16[1,2048,768]{2,1,0:T(8,128)(2,1)S(1)} %copy-done.2), kind=kOutput, calls=%fused_computation.11 | convolution fusion | flops 4026531840 | bytes 12320768 | tf_op jit(solution)/shard_map/dot_general | solution.py:10
  150.7 0.0 copy-done.3
  150.7 4.8 %fusion.3 = bf16[1280,768]{1,0:T(8,128)(2,1)S(1)} fusion(bf16[1280,2048]{1,0:T(8,128)(2,1)S(1)} %bitcast.43, f32[1280,768]{1,0:T(8,128)S(1)} %fusion.6, bf16[1,2048,768]{2,1,0:T(8,128)(2,1)S(1)} %copy-done.3), kind=kOutput, calls=%fused_computation.8 | convolution fusion | flops 4032430080 | bytes 14286848 | tf_op jit(solution)/shard_map/dot_general | solution.py:11
  155.5 6.1 %convolution_convert_fusion = bf16[1280,2048]{1,0:T(8,128)(2,1)} fusion(bf16[1280,768]{1,0:T(8,128)(2,1)S(1)} %fusion.3, bf16[1,768,2048]{2,1,0:T(8,128)(2,1)S(1)} %copy-done), kind=kOutput, calls=%fused_computation.4 | convolution fusion | flops 4029153280 | bytes 10354688 | tf_op jit(solution)/shard_map/dot_general | solution.py:13
  161.6 3.9 %all-to-all-start.1 = ((bf16[32,1,40,2048]{3,2,1,0:T(8,128)(2,1)}), bf16[32,1,40,2048]{3,2,1,0:T(8,128)(2,1)}, u32[]{:S(2)}, u32[]{:S(2)}) async-start(bf16[32,1,40,2048]{3,2,1,0:T(8,128)(2,1)} %bitcast.41), calls=%async_computation.1 | async-start | bytes 10485760 | tf_op jit(solution)/shard_map/all_to_all | solution.py:42
  165.5 0.1 copy.14
  165.6 117.0 %all-to-all-done.1 = bf16[32,1,40,2048]{3,2,1,0:T(8,128)(2,1)} async-done(((bf16[32,1,40,2048]{3,2,1,0:T(8,128)(2,1)}), bf16[32,1,40,2048]{3,2,1,0:T(8,128)(2,1)}, u32[]{:S(2)}, u32[]{:S(2)}) %all-to-all-start.1) | async-done | bytes 5242912 | tf_op jit(solution)/shard_map/all_to_all | solution.py:42
  282.7 12.0 %gather_fusion = bf16[1024,2048]{1,0:T(8,128)(2,1)} fusion(bf16[1280,2048]{1,0:T(8,128)(2,1)} %bitcast.12, s32[1024]{0:T(1024)S(1)} %broadcast_clamp_fusion), kind=kCustom, calls=%fused_computation | custom fusion | bytes 8392704 | tf_op jit(solution)/shard_map/gather | solution.py:44
  294.7 7.3 %fusion = bf16[128,2048]{1,0:T(8,128)(2,1)} fusion(bf16[1024,2048]{1,0:T(8,128)(2,1)} %gather_fusion, f32[128,8]{1,0:T(8,128)S(1)} %copy.14), kind=kLoop, calls=%fused_computation.3 | loop fusion | flops 6029312 | bytes 4722688 | tf_op jit(solution)/shard_map/reduce_sum | solution.py:45
  (11 shorter events, 0.1 us)
Async XLA Ops:
  0.0 155.5 %copy-start = (bf16[1,768,2048]{2,1,0:T(8,128)(2,1)S(1)}, bf16[1,768,2048]{2,1,0:T(8,128)(2,1)}, u32[]{:S(2)}) copy-start(bf16[1,768,2048]{2,1,0:T(8,128)(2,1)} %param.11) | copy-start | bytes 9437188
  21.6 124.7 %copy-start.2 = (bf16[1,2048,768]{2,1,0:T(8,128)(2,1)S(1)}, bf16[1,2048,768]{2,1,0:T(8,128)(2,1)}, u32[]{:S(2)}) copy-start(bf16[1,2048,768]{2,1,0:T(8,128)(2,1)} %param.9) | copy-start | bytes 9437188
  146.3 4.3 %copy-start.3 = (bf16[1,2048,768]{2,1,0:T(8,128)(2,1)S(1)}, bf16[1,2048,768]{2,1,0:T(8,128)(2,1)}, u32[]{:S(2)}) copy-start(bf16[1,2048,768]{2,1,0:T(8,128)(2,1)} %param.10) | copy-start | bytes 9437188
  161.6 3.9 %copy-start.1 = (f32[128,8]{0,1:T(8,128)S(1)}, f32[128,8]{0,1:T(8,128)}, u32[]{:S(2)}) copy-start(f32[128,8]{0,1:T(8,128)} %param.8) | copy-start | bytes 12292
  161.6 121.1 %all-to-all-start.1 = ((bf16[32,1,40,2048]{3,2,1,0:T(8,128)(2,1)}), bf16[32,1,40,2048]{3,2,1,0:T(8,128)(2,1)}, u32[]{:S(2)}, u32[]{:S(2)}) async-start(bf16[32,1,40,2048]{3,2,1,0:T(8,128)(2,1)} %bitcast.41), calls=%async_computation.1 | async-start | bytes 10485760 | tf_op jit(solution)/shard_map/all_to_all | solution.py:42
where the time goes:
time: 302 us
  blocking collectives  125 us (41%)
  waiting for transfers between devices  117 us (39%)
  local copies, waits for them, and re-layouts  23.9 us (8%)
  other arithmetic  17.2 us (6%)
  matrix products  15.2 us (5%)
  starting transfers between devices  3.93 us (1%)
    all_to_all x1, blocking collectives, body(): lax.all_to_all(outgoing, ('row', 'col'), split_axis=0, concat_axis=0, til...  125 us
    all_to_all x1, waiting for transfers between devices, body(): lax.all_to_all(produced, ('row', 'col'), split_axis=0, concat_axis=0, til...  117 us
    gather x1, local copies, waits for them, and re-layouts, body(): returned[target].reshape(tok_rows, choices_per, width).astype(jnp.float32)  12 us
    scatter x1, local copies, waits for them, and re-layouts, body(): jnp.zeros((expert_count * slot_count, width), jnp.bfloat16).at[target]  10.1 us
    another operation x2, other arithmetic  9.04 us
    reduce_sum x1, other arithmetic, body(): mixed = jnp.sum(gate_probs[:, :, None] * picked, axis=1)  7.32 us
    dot_general x1, matrix products, apply_experts(): jnp.dot(hidden, w_down[0], preferred_element_type=jnp.float32)  6.05 us
  transfers between devices with their start and end apart: 1, of which 1 were waited for; matrix products, arithmetic and copies ran while one was open for 0% of the time, Pallas kernels for 0%

commit v1 on v0

v1 whole, which is shorter than its diff:
```python
import functools
import math

import jax
import jax.numpy as jnp
from jax import lax
from jax.experimental import pallas as pl
from jax.experimental.pallas import tpu as pltpu
from jax.sharding import PartitionSpec as P

MESH = pl.DeviceIdType.MESH
BF16 = jnp.bfloat16
F32 = jnp.float32


def moe_kernel(
    rows, cols, slots, group,
    meta_in, tok_in, wg_in, wu_in, wd_in, out_ref,
    meta, tok, wg, wu, wd, disp, comb, hid, xs, xr, yr, pr, acc, zs, zr,
    load_sem, meta_send, meta_recv, ztok_send, ztok_recv, ctok_send, ctok_recv,
    x_send, x_recv, y_send, y_recv, p_send, p_recv, z_send, z_recv,
):
    r = lax.axis_index("row")
    c = lax.axis_index("col")
    chips = cols // 2
    chip, core = c // 2, c % 2
    mate = 2 * chip + (1 - core)
    count, width = tok_in.shape
    per = group // 2
    chunks = chips // per
    part = group * slots
    total = rows * part
    hidden = wg.shape[1]
    f_tile = math.gcd(hidden, 256)
    d_tile = math.gcd(width, 512)

    def remote(src, dst, send, recv, row, col):
        return pltpu.make_async_remote_copy(
            src_ref=src, dst_ref=dst, send_sem=send, recv_sem=recv,
            device_id=(row, col), device_id_type=MESH,
        )

    load_tok = pltpu.make_async_copy(tok_in, tok.at[0, 0], load_sem.at[0])
    load_meta = pltpu.make_async_copy(meta_in, meta.at[0], load_sem.at[1])
    load_w = [
        pltpu.make_async_copy(wg_in.at[0], wg, load_sem.at[2]),
        pltpu.make_async_copy(wu_in.at[0], wu, load_sem.at[3]),
        pltpu.make_async_copy(wd_in.at[0], wd, load_sem.at[4]),
    ]
    load_tok.start()
    load_meta.start()

    barrier = pltpu.get_barrier_semaphore()
    for d in range(1, cols):
        pl.semaphore_signal(barrier, inc=1, device_id=(r, (c + d) % cols), device_id_type=MESH)
    for j in range(1, rows):
        pl.semaphore_signal(barrier, inc=1, device_id=((r + j) % rows, c), device_id_type=MESH)
    pl.semaphore_wait(barrier, cols - 1 + rows - 1)

    load_tok.wait()
    tok_out = remote(tok.at[0, 0], tok.at[0, 1], ctok_send.at[0], ctok_recv.at[0], r, mate)
    tok_out.start()
    load_meta.wait()
    meta_out = []
    for d in range(1, cols):
        far, other = d // 2, d % 2
        target = 2 * ((chip + chips - far) % chips) + (core if other == 0 else 1 - core)
        copy = remote(meta.at[0], meta.at[d], meta_send.at[d], meta_recv.at[d], r, target)
        copy.start()
        meta_out.append(copy)
    ztok = [None]
    for d in range(1, chips):
        target = 2 * ((chip + chips - d) % chips) + core
        copy = remote(tok.at[0, 0], tok.at[d, 0], ztok_send.at[d], ztok_recv.at[d], r, target)
        copy.start()
        ztok.append(copy)
    for copy in load_w:
        copy.start()
    ctok = [tok_out] + [
        remote(tok.at[d, 0], tok.at[d, 1], ctok_send.at[d], ctok_recv.at[d], r, mate)
        for d in range(1, chips)
    ]
    for copy in meta_out:
        copy.wait()

    earlier = (
        lax.broadcasted_iota(jnp.int32, (count, count), 0)
        < lax.broadcasted_iota(jnp.int32, (count, count), 1)
    ).astype(BF16)
    slot_of = lax.broadcasted_iota(jnp.int32, (part, count), 0).astype(F32)
    lane_rows = 16
    row_id = lax.broadcasted_iota(jnp.int32, (lane_rows, count), 0)
    choices = meta_in.shape[0] // 2

    def route(i):
        for s in range(group):
            m = meta[i * group + s]
            ids, probs = m[:choices], m[choices:]
            named = jnp.zeros((lane_rows, count), F32)
            weights = []
            for j in range(rows):
                expert = (((r + j) % rows) * cols + c).astype(F32)
                hit = (ids == expert).astype(F32)
                named = jnp.where(row_id == j, jnp.sum(hit, axis=0, keepdims=True), named)
                weights.append(jnp.sum(hit * probs, axis=0, keepdims=True))
            rank = jnp.dot(named.astype(BF16), earlier, preferred_element_type=F32)
            key = jnp.where(named > 0.5, rank + float(s * slots), -1.0)
            for j in range(rows):
                one = (slot_of == key[j:j + 1, :]).astype(F32)
                disp[j * part:(j + 1) * part, s * count:(s + 1) * count] = one.astype(BF16)
                comb[i, j * part:(j + 1) * part, s * count:(s + 1) * count] = (
                    one * weights[j]
                ).astype(BF16)

    x_out, y_out, p_out, z_out = {}, {}, {}, {}

    def dispatch(i):
        for d in range(i * per, (i + 1) * per):
            if d > 0:
                ztok[d].wait_recv()
                ctok[d].start()
        route(i)
        for d in range(i * per, (i + 1) * per):
            ctok[d].wait_recv()

        def tile(n, _):
            at = pl.ds(pl.multiple_of(n * d_tile, d_tile), d_tile)
            block = tok[i * per:(i + 1) * per, :, :, at].reshape(group * count, d_tile)
            res = jnp.dot(disp[...], block, preferred_element_type=F32).astype(BF16)
            xr[i, 0, :, at] = res[:part]
            xs[i, :, :, at] = res[part:].reshape(rows - 1, part, d_tile)
            return 0

        lax.fori_loop(0, width // d_tile, tile, 0)
        for j in range(1, rows):
            copy = remote(
                xs.at[i, j - 1], xr.at[i, j], x_send.at[i, j], x_recv.at[i, j],
                (r + j) % rows, c,
            )
            copy.start()
            x_out[i, j] = copy

    def experts(i, first):
        for j in range(1, rows):
            x_out[i, j].wait()
        if first:
            for copy in load_w:
                copy.wait()

        def up_tile(n, _):
            at = pl.ds(pl.multiple_of(n * f_tile, f_tile), f_tile)
            x = xr[i].reshape(total, width)
            gate = jnp.dot(x, wg[:, at], preferred_element_type=F32)
            up = jnp.dot(x, wu[:, at], preferred_element_type=F32)
            hid[:, at] = (gate / (1.0 + jnp.exp(-gate)) * up).astype(BF16)
            return 0

        lax.fori_loop(0, hidden // f_tile, up_tile, 0)

        def down_tile(n, _):
            at = pl.ds(pl.multiple_of(n * d_tile, d_tile), d_tile)
            res = jnp.dot(hid[...], wd[:, at], preferred_element_type=F32).astype(BF16)
            yr[i, 0, :, at] = res[:part]
            xs[i, :, :, at] = res[part:].reshape(rows - 1, part, d_tile)
            return 0

        lax.fori_loop(0, width // d_tile, down_tile, 0)
        for j in range(1, rows):
            copy = remote(
                xs.at[i, j - 1], yr.at[i, j], y_send.at[i, j], y_recv.at[i, j],
                (r + rows - j) % rows, c,
            )
            copy.start()
            y_out[i, j] = copy

    def combine(i):
        for j in range(1, rows):
            y_out[i, j].wait()

        def tile(n, _):
            at = pl.ds(pl.multiple_of(n * d_tile, d_tile), d_tile)
            y = yr[i, :, :, at].reshape(total, d_tile)
            res = lax.dot_general(
                comb[i], y, (((0,), (0,)), ((), ())), preferred_element_type=F32
            )
            for p in range(per):
                d = i * per + p
                acc[d, :, at] = res[2 * p * count:(2 * p + 1) * count]
                tok[d, 1, :, at] = res[(2 * p + 1) * count:(2 * p + 2) * count].astype(BF16)
            return 0

        lax.fori_loop(0, width // d_tile, tile, 0)
        for d in range(i * per, (i + 1) * per):
            copy = remote(tok.at[d, 1], pr.at[d], p_send.at[d], p_recv.at[d], r, mate)
            copy.start()
            p_out[d] = copy

    def reduce_cores(i):
        for d in range(i * per, (i + 1) * per):
            p_out[d].wait()
            if d == 0:
                continue
            zs[d - 1] = (acc[d] + pr[d].astype(F32)).astype(BF16)
            copy = remote(
                zs.at[d - 1], zr.at[chips - d - 1], z_send.at[d], z_recv.at[chips - d],
                r, 2 * ((chip + d) % chips) + core,
            )
            copy.start()
            z_out[d] = copy

    order = list(range(1, chunks)) + [0]
    dispatch(0)
    for i in range(1, chunks):
        dispatch(i)
        if i > 1:
            experts(order[i - 2], i == 2)
    for n in range(max(chunks - 2, 0), chunks):
        experts(order[n], n == 0)
    for n in range(chunks):
        combine(order[n])
        if n > 0:
            reduce_cores(order[n - 1])
    reduce_cores(order[-1])
    for d in range(1, chips):
        z_out[d].wait()
    for d in range(1, chips):
        ztok[d].wait_send()
    for d in range(chips):
        ctok[d].wait_send()
    result = acc[0] + pr[0].astype(F32)
    for d in range(1, chips):
        result = result + zr[d - 1].astype(F32)
    out_ref[...] = result.astype(BF16)


def body(tokens, expert_ids, gate_probs, w_gate, w_up, w_down):
    count, choices = expert_ids.shape
    width = tokens.shape[1]
    hidden = w_gate.shape[2]
    rows = lax.axis_size("row")
    cols = lax.axis_size("col")
    slots = 5 * count * choices // (4 * rows * cols * w_gate.shape[0])
    group = 2
    while group * slots % 16:
        group *= 2
    chips = cols // 2
    chunks = cols // group
    part = group * slots
    meta = jnp.concatenate([expert_ids.astype(F32).T, gate_probs.T], axis=0)
    any_spec = pl.BlockSpec(memory_space=pl.ANY)
    dma = pltpu.SemaphoreType.DMA
    scratch = [
        pltpu.VMEM((cols, 2 * choices, count), F32),
        pltpu.VMEM((chips, 2, count, width), BF16),
        pltpu.VMEM((width, hidden), BF16),
        pltpu.VMEM((width, hidden), BF16),
        pltpu.VMEM((hidden, width), BF16),
        pltpu.VMEM((rows * part, group * count), BF16),
        pltpu.VMEM((chunks, rows * part, group * count), BF16),
        pltpu.VMEM((rows * part, hidden), BF16),
        pltpu.VMEM((chunks, rows - 1, part, width), BF16),
        pltpu.VMEM((chunks, rows, part, width), BF16),
        pltpu.VMEM((chunks, rows, part, width), BF16),
        pltpu.VMEM((chips, count, width), BF16),
        pltpu.VMEM((chips, count, width), F32),
        pltpu.VMEM((chips - 1, count, width), BF16),
        pltpu.VMEM((chips - 1, count, width), BF16),
        dma((5,)),
        dma((cols,)), dma((cols,)),
        dma((chips,)), dma((chips,)),
        dma((chips,)), dma((chips,)),
        dma((chunks, rows)), dma((chunks, rows)),
        dma((chunks, rows)), dma((chunks, rows)),
        dma((chips,)), dma((chips,)),
        dma((chips,)), dma((chips,)),
    ]
    return pl.pallas_call(
        functools.partial(moe_kernel, rows, cols, slots, group),
        out_shape=jax.ShapeDtypeStruct((count, width), BF16),
        in_specs=[any_spec] * 5,
        out_specs=pl.BlockSpec(memory_space=pltpu.VMEM),
        scratch_shapes=scratch,
        compiler_params=pltpu.CompilerParams(
            collective_id=0, has_side_effects=True, vmem_limit_bytes=67043328
        ),
    )(meta, tokens, w_gate, w_up, w_down)


def solution(mesh):
    in_specs = (
        P(("row", "col"), None),
        P(("row", "col"), None),
        P(("row", "col"), None),
        P(("row", "col"), None, None),
        P(("row", "col"), None, None),
        P(("row", "col"), None, None),
    )
    out_specs = P(("row", "col"), None)
    return jax.shard_map(body, mesh=mesh, in_specs=in_specs, out_specs=out_specs, check_vma=False)
```

time: 302 us -> 172 us (0.57)
  the two profiles are of different devices: /device:TPU:0 before, /device:TPU:27 now
where the time goes in v1:
time: 172 us
  Pallas kernels  168 us (98%)
  other arithmetic  1.97 us (1%)
  local copies, waits for them, and re-layouts  1.88 us (1%)
    pallas_call x1, Pallas kernels, body(): pl.pallas_call(functools.partial(moe_kernel, rows, cols, slots, group), o...  168 us

profile of v1, /device:TPU:27, one launch (start us, length us, event | category | flops | bytes accessed | tf_op | source)
XLA Modules:
  0.0 171.8 jit_solution(8517242898418295930)
XLA Ops:
  0.0 0.7 convert_bitcast_fusion
  0.7 1.3 pad_maximum_fusion.meta_in
  2.0 168.0 %shard_map.64 = bf16[128,2048]{1,0:T(8,128)(2,1)} custom-call(f32[16,128]{1,0:T(8,128)} %pad_maximum_fusion.meta_in, bf16[128,2048]{1,0:T(8,128)(2,1)} %tok_in.1, bf16[1,2048,768]{2,1,0:T(8,128)(2,1)} %wg_in.1, bf16[1,2048,768]{2,1,0:T(8,128)(2,1)} %wu_in.1, bf16[1,768,2048]{2,1,0:T(8,128)(2,1)} %wd_in.1), custom_call_target="tpu_custom_call" | custom-call | tf_op jit(solution)/shard_map/pallas_call | solution.py:277
  170.0 1.9 %copy.8 = bf16[128,2048]{1,0:T(8,128)(2,1)} copy(bf16[128,2048]{1,0:T(8,128)(2,1)} %shard_map.64) | data formatting | bytes 1048576

commit v2 on v1

--- a/solution.py
+++ b/solution.py
@@ -40,8 +40,18 @@
             device_id=(row, col), device_id_type=MESH,
         )
 
-    load_tok = pltpu.make_async_copy(tok_in, tok.at[0, 0], load_sem.at[0])
-    load_meta = pltpu.make_async_copy(meta_in, meta.at[0], load_sem.at[1])
+    short = jnp.minimum(chip, chips - 1 - chip)
+    side = jnp.where(2 * chip < chips, 1, -1)
+    order, signs = [chip], [None]
+    for p in range(1, chips):
+        both = p <= 2 * short
+        sign = jnp.where(both, 1 if p % 2 else -1, side)
+        far = jnp.where(both, (p + 1) // 2, p - short)
+        order.append(chip + sign * far)
+        signs.append(sign)
+
+    load_tok = pltpu.make_async_copy(tok_in, tok.at[chip, 0], load_sem.at[0])
+    load_meta = pltpu.make_async_copy(meta_in, meta.at[chip, 0], load_sem.at[1])
     load_w = [
         pltpu.make_async_copy(wg_in.at[0], wg, load_sem.at[2]),
         pltpu.make_async_copy(wu_in.at[0], wu, load_sem.at[3]),
@@ -57,31 +67,51 @@
         pl.semaphore_signal(barrier, inc=1, device_id=((r + j) % rows, c), device_id_type=MESH)
     pl.semaphore_wait(barrier, cols - 1 + rows - 1)
 
+    def hop(q, send, to):
+        return remote(
+            tok.at[q, 0], tok.at[q, 0], ztok_send.at[send], ztok_recv.at[q],
+            r, 2 * ((to + chips) % chips) + core,
+        )
+
+    def onward(p, act):
+        if p == 0:
+            @pl.when(chip > 0)
+            def _():
+                act(hop(chip, 0, chip - 1))
+
+            @pl.when(chip < chips - 1)
+            def _():
+                act(hop(chip, chips, chip + 1))
+        else:
+            to = chip - signs[p]
+
+            @pl.when((to >= 0) & (to < chips))
+            def _():
+                act(hop(order[p], p, to))
+
+    ctok = [
+        remote(tok.at[q, 0], tok.at[q, 1], ctok_send.at[p], ctok_recv.at[p], r, mate)
+        for p, q in enumerate(order)
+    ]
     load_tok.wait()
-    tok_out = remote(tok.at[0, 0], tok.at[0, 1], ctok_send.at[0], ctok_recv.at[0], r, mate)
-    tok_out.start()
+    ctok[0].start()
     load_meta.wait()
-    meta_out = []
+
+    def meta_copy(d, t, slot):
+        far, other = d // 2, d % 2
+        return remote(
+            meta.at[chip, 0], meta.at[slot, other], meta_send.at[d], meta_recv.at[slot, other],
+            r, 2 * t + (core if other == 0 else 1 - core),
+        )
+
     for d in range(1, cols):
-        far, other = d // 2, d % 2
-        target = 2 * ((chip + chips - far) % chips) + (core if other == 0 else 1 - core)
-        copy = remote(meta.at[0], meta.at[d], meta_send.at[d], meta_recv.at[d], r, target)
-        copy.start()
-        meta_out.append(copy)
-    ztok = [None]
-    for d in range(1, chips):
-        target = 2 * ((chip + chips - d) % chips) + core
-        copy = remote(tok.at[0, 0], tok.at[d, 0], ztok_send.at[d], ztok_recv.at[d], r, target)
-        copy.start()
-        ztok.append(copy)
+        meta_copy(d, (chip + d // 2) % chips, chip).start()
+    onward(0, lambda copy: copy.start())
     for copy in load_w:
         copy.start()
-    ctok = [tok_out] + [
-        remote(tok.at[d, 0], tok.at[d, 1], ctok_send.at[d], ctok_recv.at[d], r, mate)
-        for d in range(1, chips)
-    ]
-    for copy in meta_out:
-        copy.wait()
+    for d in range(1, cols):
+        t = (chip + d // 2) % chips
+        meta_copy(d, t, t).wait()
 
     earlier = (
         lax.broadcasted_iota(jnp.int32, (count, count), 0)
@@ -94,7 +124,7 @@
 
     def route(i):
         for s in range(group):
-            m = meta[i * group + s]
+            m = meta[order[i * per + s // 2], s % 2]
             ids, probs = m[:choices], m[choices:]
             named = jnp.zeros((lane_rows, count), F32)
             weights = []
@@ -117,7 +147,8 @@
     def dispatch(i):
         for d in range(i * per, (i + 1) * per):
             if d > 0:
-                ztok[d].wait_recv()
+                hop(order[d], d, chip).wait_recv()
+                onward(d, lambda copy: copy.start())
                 ctok[d].start()
         route(i)
         for d in range(i * per, (i + 1) * per):
@@ -125,7 +156,9 @@
 
         def tile(n, _):
             at = pl.ds(pl.multiple_of(n * d_tile, d_tile), d_tile)
-            block = tok[i * per:(i + 1) * per, :, :, at].reshape(group * count, d_tile)
+            block = jnp.concatenate(
+                [tok[q, :, :, at].reshape(2 * count, d_tile) for q in order[i * per:(i + 1) * per]]
+            )
             res = jnp.dot(disp[...], block, preferred_element_type=F32).astype(BF16)
             xr[i, 0, :, at] = res[:part]
             xs[i, :, :, at] = res[part:].reshape(rows - 1, part, d_tile)
@@ -186,12 +219,12 @@
             for p in range(per):
                 d = i * per + p
                 acc[d, :, at] = res[2 * p * count:(2 * p + 1) * count]
-                tok[d, 1, :, at] = res[(2 * p + 1) * count:(2 * p + 2) * count].astype(BF16)
+                tok[order[d], 1, :, at] = res[(2 * p + 1) * count:(2 * p + 2) * count].astype(BF16)
             return 0
 
         lax.fori_loop(0, width // d_tile, tile, 0)
         for d in range(i * per, (i + 1) * per):
-            copy = remote(tok.at[d, 1], pr.at[d], p_send.at[d], p_recv.at[d], r, mate)
+            copy = remote(tok.at[order[d], 1], pr.at[d], p_send.at[d], p_recv.at[d], r, mate)
             copy.start()
             p_out[d] = copy
 
@@ -202,34 +235,31 @@
                 continue
             zs[d - 1] = (acc[d] + pr[d].astype(F32)).astype(BF16)
             copy = remote(
-                zs.at[d - 1], zr.at[chips - d - 1], z_send.at[d], z_recv.at[chips - d],
-                r, 2 * ((chip + d) % chips) + core,
+                zs.at[d - 1], zr.at[chip], z_send.at[d], z_recv.at[chip], r, 2 * order[d] + core
             )
             copy.start()
             z_out[d] = copy
 
-    order = list(range(1, chunks)) + [0]
+    turn = list(range(1, chunks)) + [0]
     dispatch(0)
     for i in range(1, chunks):
         dispatch(i)
         if i > 1:
-            experts(order[i - 2], i == 2)
+            experts(turn[i - 2], i == 2)
     for n in range(max(chunks - 2, 0), chunks):
-        experts(order[n], n == 0)
+        experts(turn[n], n == 0)
     for n in range(chunks):
-        combine(order[n])
-        if n > 0:
-            reduce_cores(order[n - 1])
-    reduce_cores(order[-1])
-    for d in range(1, chips):
-        z_out[d].wait()
-    for d in range(1, chips):
-        ztok[d].wait_send()
-    for d in range(chips):
-        ctok[d].wait_send()
+        combine(turn[n])
+        reduce_cores(turn[n])
     result = acc[0] + pr[0].astype(F32)
     for d in range(1, chips):
-        result = result + zr[d - 1].astype(F32)
+        q = order[d]
+        z_out[d].wait_send()
+        remote(zs.at[d - 1], zr.at[q], z_send.at[d], z_recv.at[q], r, 2 * q + core).wait_recv()
+        result = result + zr[q].astype(F32)
+    for d in range(chips):
+        onward(d, lambda copy: copy.wait_send())
+        ctok[d].wait_send()
     out_ref[...] = result.astype(BF16)
 
 
@@ -250,7 +280,7 @@
     any_spec = pl.BlockSpec(memory_space=pl.ANY)
     dma = pltpu.SemaphoreType.DMA
     scratch = [
-        pltpu.VMEM((cols, 2 * choices, count), F32),
+        pltpu.VMEM((chips, 2, 2 * choices, count), F32),
         pltpu.VMEM((chips, 2, count, width), BF16),
         pltpu.VMEM((width, hidden), BF16),
         pltpu.VMEM((width, hidden), BF16),
@@ -264,10 +294,10 @@
         pltpu.VMEM((chips, count, width), BF16),
         pltpu.VMEM((chips, count, width), F32),
         pltpu.VMEM((chips - 1, count, width), BF16),
-        pltpu.VMEM((chips - 1, count, width), BF16),
+        pltpu.VMEM((chips, count, width), BF16),
         dma((5,)),
-        dma((cols,)), dma((cols,)),
-        dma((chips,)), dma((chips,)),
+        dma((cols,)), dma((chips, 2)),
+        dma((chips + 1,)), dma((chips,)),
         dma((chips,)), dma((chips,)),
         dma((chunks, rows)), dma((chunks, rows)),
         dma((chunks, rows)), dma((chunks, rows)),

time: 172 us -> 155 us (0.901)
  the two profiles are of different devices: /device:TPU:27 before, /device:TPU:0 now
where the time goes in v2:
time: 155 us
  Pallas kernels  151 us (97%)
  other arithmetic  1.97 us (1%)
  local copies, waits for them, and re-layouts  1.88 us (1%)
    pallas_call x1, Pallas kernels, body(): pl.pallas_call(functools.partial(moe_kernel, rows, cols, slots, group), o...  151 us

profile of v2, /device:TPU:0, one launch (start us, length us, event | category | flops | bytes accessed | tf_op | source)
XLA Modules:
  0.0 154.9 jit_solution(14219998561397818568)
XLA Ops:
  0.0 0.7 convert_bitcast_fusion
  0.7 1.3 pad_maximum_fusion.meta_in
  2.0 151.0 %shard_map.64 = bf16[128,2048]{1,0:T(8,128)(2,1)} custom-call(f32[16,128]{1,0:T(8,128)} %pad_maximum_fusion.meta_in, bf16[128,2048]{1,0:T(8,128)(2,1)} %tok_in.1, bf16[1,2048,768]{2,1,0:T(8,128)(2,1)} %wg_in.1, bf16[1,2048,768]{2,1,0:T(8,128)(2,1)} %wu_in.1, bf16[1,768,2048]{2,1,0:T(8,128)(2,1)} %wd_in.1), custom_call_target="tpu_custom_call" | custom-call | tf_op jit(solution)/shard_map/pallas_call | solution.py:307
  153.0 1.9 %copy.8 = bf16[128,2048]{1,0:T(8,128)(2,1)} copy(bf16[128,2048]{1,0:T(8,128)(2,1)} %shard_map.64) | data formatting | bytes 1048576

commit v3 on v2

--- a/solution.py
+++ b/solution.py
@@ -11,13 +11,14 @@
 MESH = pl.DeviceIdType.MESH
 BF16 = jnp.bfloat16
 F32 = jnp.float32
+PIECES = 2
 
 
 def moe_kernel(
-    rows, cols, slots, group,
-    meta_in, tok_in, wg_in, wu_in, wd_in, out_ref,
-    meta, tok, wg, wu, wd, disp, comb, hid, xs, xr, yr, pr, acc, zs, zr,
-    load_sem, meta_send, meta_recv, ztok_send, ztok_recv, ctok_send, ctok_recv,
+    rows, cols, slots, group, pieces,
+    ids_in, probs_in, tok_in, wg_in, wu_in, wd_in, out_ref,
+    ids_all, probs_all, tok, wg, wu, wd, disp, comb, hid, xs, xr, yr, pr, acc, zs, zr,
+    load_sem, ids_send, ids_recv, probs_send, probs_recv, ztok_send, ztok_recv, ctok_send, ctok_recv,
     x_send, x_recv, y_send, y_recv, p_send, p_recv, z_send, z_recv,
 ):
     r = lax.axis_index("row")
@@ -32,7 +33,8 @@
     total = rows * part
     hidden = wg.shape[1]
     f_tile = math.gcd(hidden, 256)
-    d_tile = math.gcd(width, 512)
+    d_tile = math.gcd(width // pieces, 512)
+    piece = width // pieces
 
     def remote(src, dst, send, recv, row, col):
         return pltpu.make_async_remote_copy(
@@ -51,14 +53,16 @@
         signs.append(sign)
 
     load_tok = pltpu.make_async_copy(tok_in, tok.at[chip, 0], load_sem.at[0])
-    load_meta = pltpu.make_async_copy(meta_in, meta.at[chip, 0], load_sem.at[1])
+    load_ids = pltpu.make_async_copy(ids_in, ids_all.at[chip, 0], load_sem.at[1])
+    load_probs = pltpu.make_async_copy(probs_in, probs_all.at[chip, 0], load_sem.at[5])
     load_w = [
         pltpu.make_async_copy(wg_in.at[0], wg, load_sem.at[2]),
         pltpu.make_async_copy(wu_in.at[0], wu, load_sem.at[3]),
         pltpu.make_async_copy(wd_in.at[0], wd, load_sem.at[4]),
     ]
     load_tok.start()
-    load_meta.start()
+    load_ids.start()
+    load_probs.start()
 
     barrier = pltpu.get_barrier_semaphore()
     for d in range(1, cols):
@@ -95,23 +99,33 @@
     ]
     load_tok.wait()
     ctok[0].start()
-    load_meta.wait()
-
-    def meta_copy(d, t, slot):
+    load_ids.wait()
+    load_probs.wait()
+
+    def routing(d, t, slot):
         far, other = d // 2, d % 2
-        return remote(
-            meta.at[chip, 0], meta.at[slot, other], meta_send.at[d], meta_recv.at[slot, other],
-            r, 2 * t + (core if other == 0 else 1 - core),
+        to = 2 * t + (core if other == 0 else 1 - core)
+        return (
+            remote(
+                ids_all.at[chip, 0], ids_all.at[slot, other],
+                ids_send.at[d], ids_recv.at[slot, other], r, to,
+            ),
+            remote(
+                probs_all.at[chip, 0], probs_all.at[slot, other],
+                probs_send.at[d], probs_recv.at[slot, other], r, to,
+            ),
         )
 
     for d in range(1, cols):
-        meta_copy(d, (chip + d // 2) % chips, chip).start()
+        for copy in routing(d, (chip + d // 2) % chips, chip):
+            copy.start()
     onward(0, lambda copy: copy.start())
     for copy in load_w:
         copy.start()
     for d in range(1, cols):
         t = (chip + d // 2) % chips
-        meta_copy(d, t, t).wait()
+        for copy in routing(d, t, t):
+            copy.wait()
 
     earlier = (
         lax.broadcasted_iota(jnp.int32, (count, count), 0)
@@ -120,16 +134,15 @@
     slot_of = lax.broadcasted_iota(jnp.int32, (part, count), 0).astype(F32)
     lane_rows = 16
     row_id = lax.broadcasted_iota(jnp.int32, (lane_rows, count), 0)
-    choices = meta_in.shape[0] // 2
 
     def route(i):
         for s in range(group):
-            m = meta[order[i * per + s // 2], s % 2]
-            ids, probs = m[:choices], m[choices:]
+            ids = ids_all[order[i * per + s // 2], s % 2]
+            probs = probs_all[order[i * per + s // 2], s % 2]
             named = jnp.zeros((lane_rows, count), F32)
             weights = []
             for j in range(rows):
-                expert = (((r + j) % rows) * cols + c).astype(F32)
+                expert = ((r + j) % rows) * cols + c
                 hit = (ids == expert).astype(F32)
                 named = jnp.where(row_id == j, jnp.sum(hit, axis=0, keepdims=True), named)
                 weights.append(jnp.sum(hit * probs, axis=0, keepdims=True))
@@ -197,18 +210,20 @@
             xs[i, :, :, at] = res[part:].reshape(rows - 1, part, d_tile)
             return 0
 
-        lax.fori_loop(0, width // d_tile, down_tile, 0)
+        for h in range(pieces):
+            at = pl.ds(h * piece, piece)
+            lax.fori_loop(h * piece // d_tile, (h + 1) * piece // d_tile, down_tile, 0)
+            for j in range(1, rows):
+                copy = remote(
+                    xs.at[i, j - 1, :, at], yr.at[i, j, :, at],
+                    y_send.at[i, j, h], y_recv.at[i, j, h], (r + rows - j) % rows, c,
+                )
+                copy.start()
+                y_out[i, j, h] = copy
+
+    def combine(i, h):
         for j in range(1, rows):
-            copy = remote(
-                xs.at[i, j - 1], yr.at[i, j], y_send.at[i, j], y_recv.at[i, j],
-                (r + rows - j) % rows, c,
-            )
-            copy.start()
-            y_out[i, j] = copy
-
-    def combine(i):
-        for j in range(1, rows):
-            y_out[i, j].wait()
+            y_out[i, j, h].wait()
 
         def tile(n, _):
             at = pl.ds(pl.multiple_of(n * d_tile, d_tile), d_tile)
@@ -222,45 +237,50 @@
                 tok[order[d], 1, :, at] = res[(2 * p + 1) * count:(2 * p + 2) * count].astype(BF16)
             return 0
 
-        lax.fori_loop(0, width // d_tile, tile, 0)
+        lax.fori_loop(h * piece // d_tile, (h + 1) * piece // d_tile, tile, 0)
+        at = pl.ds(h * piece, piece)
         for d in range(i * per, (i + 1) * per):
-            copy = remote(tok.at[order[d], 1], pr.at[d], p_send.at[d], p_recv.at[d], r, mate)
-            copy.start()
-            p_out[d] = copy
-
-    def reduce_cores(i):
-        for d in range(i * per, (i + 1) * per):
-            p_out[d].wait()
-            if d == 0:
-                continue
-            zs[d - 1] = (acc[d] + pr[d].astype(F32)).astype(BF16)
             copy = remote(
-                zs.at[d - 1], zr.at[chip], z_send.at[d], z_recv.at[chip], r, 2 * order[d] + core
+                tok.at[order[d], 1, :, at], pr.at[d, :, at], p_send.at[d, h], p_recv.at[d, h],
+                r, mate,
             )
             copy.start()
-            z_out[d] = copy
-
-    turn = list(range(1, chunks)) + [0]
-    dispatch(0)
-    for i in range(1, chunks):
+            p_out[d, h] = copy
+
+    def partial_copy(d, h, slot):
+        at = pl.ds(h * piece, piece)
+        return remote(
+            zs.at[d - 1, :, at], zr.at[slot, :, at], z_send.at[d, h], z_recv.at[slot, h],
+            r, 2 * order[d] + core,
+        )
+
+    def reduce_cores(i, h):
+        at = pl.ds(h * piece, piece)
+        for d in range(i * per, (i + 1) * per):
+            p_out[d, h].wait()
+            if d > 0:
+                zs[d - 1, :, at] = (acc[d, :, at] + pr[d, :, at].astype(F32)).astype(BF16)
+                partial_copy(d, h, chip).start()
+
+    turn = list(range(chunks // 2, chunks)) + list(range(chunks // 2 - 1, -1, -1))
+    for i in range(chunks):
         dispatch(i)
-        if i > 1:
-            experts(turn[i - 2], i == 2)
-    for n in range(max(chunks - 2, 0), chunks):
+    for n in range(chunks):
         experts(turn[n], n == 0)
     for n in range(chunks):
-        combine(turn[n])
-        reduce_cores(turn[n])
-    result = acc[0] + pr[0].astype(F32)
-    for d in range(1, chips):
-        q = order[d]
-        z_out[d].wait_send()
-        remote(zs.at[d - 1], zr.at[q], z_send.at[d], z_recv.at[q], r, 2 * q + core).wait_recv()
-        result = result + zr[q].astype(F32)
+        for h in range(pieces):
+            combine(turn[n], h)
+            reduce_cores(turn[n], h)
+    for h in range(pieces):
+        at = pl.ds(h * piece, piece)
+        result = acc[0, :, at] + pr[0, :, at].astype(F32)
+        for d in range(1, chips):
+            partial_copy(d, h, order[d]).wait()
+            result = result + zr[order[d], :, at].astype(F32)
+        out_ref[:, at] = result.astype(BF16)
     for d in range(chips):
         onward(d, lambda copy: copy.wait_send())
         ctok[d].wait_send()
-    out_ref[...] = result.astype(BF16)
 
 
 def body(tokens, expert_ids, gate_probs, w_gate, w_up, w_down):
@@ -276,11 +296,11 @@
     chips = cols // 2
     chunks = cols // group
     part = group * slots
-    meta = jnp.concatenate([expert_ids.astype(F32).T, gate_probs.T], axis=0)
     any_spec = pl.BlockSpec(memory_space=pl.ANY)
     dma = pltpu.SemaphoreType.DMA
     scratch = [
-        pltpu.VMEM((chips, 2, 2 * choices, count), F32),
+        pltpu.VMEM((chips, 2, choices, count), jnp.int32),
+        pltpu.VMEM((chips, 2, choices, count), F32),
         pltpu.VMEM((chips, 2, count, width), BF16),
         pltpu.VMEM((width, hidden), BF16),
         pltpu.VMEM((width, hidden), BF16),
@@ -295,25 +315,26 @@
         pltpu.VMEM((chips, count, width), F32),
         pltpu.VMEM((chips - 1, count, width), BF16),
         pltpu.VMEM((chips, count, width), BF16),
-        dma((5,)),
+        dma((6,)),
+        dma((cols,)), dma((chips, 2)),
         dma((cols,)), dma((chips, 2)),
         dma((chips + 1,)), dma((chips,)),
         dma((chips,)), dma((chips,)),
         dma((chunks, rows)), dma((chunks, rows)),
-        dma((chunks, rows)), dma((chunks, rows)),
-        dma((chips,)), dma((chips,)),
-        dma((chips,)), dma((chips,)),
+        dma((chunks, rows, PIECES)), dma((chunks, rows, PIECES)),
+        dma((chips, PIECES)), dma((chips, PIECES)),
+        dma((chips, PIECES)), dma((chips, PIECES)),
     ]
     return pl.pallas_call(
-        functools.partial(moe_kernel, rows, cols, slots, group),
+        functools.partial(moe_kernel, rows, cols, slots, group, PIECES),
         out_shape=jax.ShapeDtypeStruct((count, width), BF16),
-        in_specs=[any_spec] * 5,
+        in_specs=[any_spec] * 6,
         out_specs=pl.BlockSpec(memory_space=pltpu.VMEM),
         scratch_shapes=scratch,
         compiler_params=pltpu.CompilerParams(
             collective_id=0, has_side_effects=True, vmem_limit_bytes=67043328
         ),
-    )(meta, tokens, w_gate, w_up, w_down)
+    )(expert_ids.T, gate_probs.T, tokens, w_gate, w_up, w_down)
 
 
 def solution(mesh):

time: 155 us -> 136 us (0.88)
  Pallas kernels: 151 us -> 134 us
  other arithmetic: 1.97 us -> 0 us
    pallas_call x1, Pallas kernels: 151 us -> 134 us  [body(): pl.pallas_call(functools.partial(moe_kernel, rows, cols, slots, group, PI...]
where the time goes in v3:
time: 136 us
  Pallas kernels  134 us (99%)
  local copies, waits for them, and re-layouts  1.88 us (1%)
    pallas_call x1, Pallas kernels, body(): pl.pallas_call(functools.partial(moe_kernel, rows, cols, slots, group, PI...  134 us

profile of v3, /device:TPU:0, one launch (start us, length us, event | category | flops | bytes accessed | tf_op | source)
XLA Modules:
  0.0 136.2 jit_solution(14513121455294074704)
XLA Ops:
  0.0 134.3 %shard_map.64 = bf16[128,2048]{1,0:T(8,128)(2,1)} custom-call(s32[8,128]{1,0:T(8,128)} %bitcast.2, f32[8,128]{1,0:T(8,128)} %bitcast.3, bf16[128,2048]{1,0:T(8,128)(2,1)} %tok_in.1, bf16[1,2048,768]{2,1,0:T(8,128)(2,1)} %wg_in.1, bf16[1,2048,768]{2,1,0:T(8,128)(2,1)} %wu_in.1, bf16[1,768,2048]{2,1,0:T(8,128)(2,1)} %wd_in.1), custom_call_target="tpu_custom_call" | custom-call | tf_op jit(solution)/shard_map/pallas_call | solution.py:328
  134.3 1.9 %copy.8 = bf16[128,2048]{1,0:T(8,128)(2,1)} copy(bf16[128,2048]{1,0:T(8,128)(2,1)} %shard_map.64) | data formatting | bytes 1048576

commit v4 on v3

--- a/solution.py
+++ b/solution.py
@@ -122,11 +122,6 @@
     onward(0, lambda copy: copy.start())
     for copy in load_w:
         copy.start()
-    for d in range(1, cols):
-        t = (chip + d // 2) % chips
-        for copy in routing(d, t, t):
-            copy.wait()
-
     earlier = (
         lax.broadcasted_iota(jnp.int32, (count, count), 0)
         < lax.broadcasted_iota(jnp.int32, (count, count), 1)
@@ -163,6 +158,9 @@
                 hop(order[d], d, chip).wait_recv()
                 onward(d, lambda copy: copy.start())
                 ctok[d].start()
+            for other in range(0 if d > 0 else 1, 2):
+                for copy in routing(other, order[d], order[d]):
+                    copy.wait_recv()
         route(i)
         for d in range(i * per, (i + 1) * per):
             ctok[d].wait_recv()
@@ -278,6 +276,9 @@
             partial_copy(d, h, order[d]).wait()
             result = result + zr[order[d], :, at].astype(F32)
         out_ref[:, at] = result.astype(BF16)
+    for d in range(1, cols):
+        for copy in routing(d, (chip + d // 2) % chips, chip):
+            copy.wait_send()
     for d in range(chips):
         onward(d, lambda copy: copy.wait_send())
         ctok[d].wait_send()

time: 136 us -> 133 us (0.978)
  Pallas kernels: 134 us -> 131 us
    pallas_call x1, Pallas kernels: 134 us -> 131 us  [body(): pl.pallas_call(functools.partial(moe_kernel, rows, cols, slots, group, PI...]
where the time goes in v4:
time: 133 us
  Pallas kernels  131 us (98%)
  local copies, waits for them, and re-layouts  1.88 us (1%)
    pallas_call x1, Pallas kernels, body(): pl.pallas_call(functools.partial(moe_kernel, rows, cols, slots, group, PI...  131 us

profile of v4, /device:TPU:0, one launch (start us, length us, event | category | flops | bytes accessed | tf_op | source)
XLA Modules:
  0.0 133.1 jit_solution(15483702862499729273)
XLA Ops:
  0.0 131.2 %shard_map.64 = bf16[128,2048]{1,0:T(8,128)(2,1)} custom-call(s32[8,128]{1,0:T(8,128)} %bitcast.2, f32[8,128]{1,0:T(8,128)} %bitcast.3, bf16[128,2048]{1,0:T(8,128)(2,1)} %tok_in.1, bf16[1,2048,768]{2,1,0:T(8,128)(2,1)} %wg_in.1, bf16[1,2048,768]{2,1,0:T(8,128)(2,1)} %wu_in.1, bf16[1,768,2048]{2,1,0:T(8,128)(2,1)} %wd_in.1), custom_call_target="tpu_custom_call" | custom-call | tf_op jit(solution)/shard_map/pallas_call | solution.py:329
  131.2 1.9 %copy.8 = bf16[128,2048]{1,0:T(8,128)(2,1)} copy(bf16[128,2048]{1,0:T(8,128)(2,1)} %shard_map.64) | data formatting | bytes 1048576
